TPU v7x, 32 devices: a whole 2x2x4 slice. The times are simulated.
32 devices in a mesh: pair: 8 (over y, x, core), aux: 4 (over z).
Axes of the slice: x: 2, y: 2, z: 4, core: 2. Of those that a mesh axis runs over, the one named last changes fastest.
Arguments:
- integrals: float32 [8, 640, 2048], P(None, 'aux', 'pair'), may hold values from -6 to 6
- factor: float32 [2048, 2048], P('aux', 'pair'), may hold values from -1 to 2, as said below
- diag_inverse: float32 [4, 512, 512], P('aux'), may hold values from -1 to 1, as said below
Outputs:
- transformed: float32 [8, 640, 2048], P('pair', None, 'aux')
Inputs may be any that keep to these rules, and one draw needn't show every extreme that they name: factor is zero above its diagonal. diag_inverse[j] is the inverse, up to rounding, of the factor's j-th diagonal block of 512 x 512.
All inputs are finite; a program needn't handle non-finite values.
Results may differ from a plain program's by a relative error of at most 0.0001.
Values sent between devices are 32-bit elements; how exact they have to be, the bound alone decides.
A program may use at most 128 MiB of HBM per device.

v0:
```python
import jax
import jax.numpy as jnp
from jax import lax
from jax.sharding import PartitionSpec as P


def from_behind(block, axis, distance):
    devices = range(lax.axis_size(axis))
    route = [(i - distance, i) for i in devices if i - distance in devices]
    return lax.ppermute(block, axis, route)


def product(left, right):
    return jnp.dot(left, right, precision=lax.Precision.HIGHEST, preferred_element_type=jnp.float32)


def local(integrals, factor, diag_inverse):
    relaid = lax.all_to_all(
        lax.all_to_all(integrals, "pair", split_axis=0, concat_axis=2, tiled=True),
        "aux",
        split_axis=2,
        concat_axis=1,
        tiled=True,
    )
    occ_count, virt_count, panel_width = relaid.shape
    remain = relaid.reshape(occ_count * virt_count, panel_width)
    row_panel = lax.all_gather(factor, "pair", axis=1, tiled=True)
    inverse_t = diag_inverse[0].T
    own_index = lax.axis_index("aux")
    panel_count = lax.axis_size("aux")
    result = jnp.zeros_like(remain)
    for step in range(panel_count):
        result = lax.cond(own_index == step, lambda: product(remain, inverse_t), lambda: result)
        if step + 1 < panel_count:
            factor_block = row_panel[:, step * panel_width : (step + 1) * panel_width].T
            travel = result
            for distance in range(1, panel_count - step):
                travel = from_behind(travel, "aux", 1)
                remain = lax.cond(
                    own_index == step + distance,
                    lambda: remain - product(travel, factor_block),
                    lambda: remain,
                )
    return result.reshape(occ_count, virt_count, panel_width)


def solution(mesh):
    in_specs = (P(None, "aux", "pair"), P("aux", "pair"), P("aux", None, None))
    out_specs = P("pair", None, "aux")
    return jax.shard_map(local, mesh=mesh, in_specs=in_specs, out_specs=out_specs, check_vma=False)
```

profile of v0, /device:TPU:30, one launch (start us, length us, event | category | flops | bytes accessed | tf_op | source)
XLA Modules:
  0.0 305.4 jit_solution(4007244110930413222)
XLA Ops:
  6.5 0.0 copy-start.2
  6.5 0.0 all-gather.2.cloned.1.call-start
  6.5 2.2 copy.20
  8.7 0.0 all-gather.2.cloned.1.call-update
  8.7 0.0 copy-done.2
  8.8 25.5 %all_to_all.33 = f32[8,160,256]{2,1,0:T(8,128)} all-to-all(f32[8,160,256]{2,1,0:T(8,128)S(1)} %copy-done.2), channel_id=1, replica_groups=mesh['pair'=8,'aux'=4] {'pair'}, dimensions={0} | all-to-all | bytes 2621440 | tf_op jit(solution)/shard_map/all_to_all | solution.py:19
  34.2 1.8 copy.21
  36.0 3.7 %reshape.15 = f32[1,160,2048]{1,0,2:T(1,128)} reshape(f32[1,160,8,256]{1,3,2,0:T(8,128)S(1)} %copy.21) | data formatting | bytes 2621440 | tf_op jit(solution)/shard_map/all_to_all | solution.py:19
  39.7 0.0 copy-start.5
  39.7 5.2 %all-to-all-start.1 = ((f32[1,160,2048]{1,0,2:T(1,128)}), f32[1,160,2048]{1,0,2:T(1,128)}, u32[]{:S(2)}, u32[]{:S(2)}) async-start(f32[1,160,2048]{1,0,2:T(1,128)} %reshape.15), calls=%async_computation.1 | async-start | bytes 4194304 | tf_op jit(solution)/shard_map/all_to_all | solution.py:18
  44.9 0.0 copy-done.5
  44.9 0.3 copy.19
  45.3 45.0 %all-to-all-done.1 = f32[1,160,2048]{1,0,2:T(1,128)} async-done(((f32[1,160,2048]{1,0,2:T(1,128)}), f32[1,160,2048]{1,0,2:T(1,128)}, u32[]{:S(2)}, u32[]{:S(2)}) %all-to-all-start.1) | async-done | bytes 1310752 | tf_op jit(solution)/shard_map/all_to_all | solution.py:18
  90.3 4.4 %copy.17 = f32[1,160,2048]{2,1,0:T(8,128)S(1)} copy(f32[1,160,2048]{1,0,2:T(1,128)} %all-to-all-done.1) | data formatting | bytes 2621440 | tf_op jit(solution)/shard_map/all_to_all | solution.py:18
  94.8 1.9 all_to_all.29
  96.7 1.7 copy.18
  98.4 1.2 conditional.10
  98.5 1.2 broadcast_in_dim.2
  99.7 1.3 collective-permute-start
  101.0 29.6 %collective-permute-done = f32[640,512]{1,0:T(8,128)S(1)} collective-permute-done((f32[640,512]{1,0:T(8,128)}, f32[640,512]{1,0:T(8,128)S(1)}, u32[]{:S(2)}, u32[]{:S(2)}) %collective-permute-start) | collective-permute-done | bytes 1310752 | tf_op jit(solution)/shard_map/ppermute | solution.py:10
  130.6 0.0 copy-start.3
  130.6 1.1 copy-done.3
  131.7 1.3 collective-permute-start.1
  133.0 28.7 %collective-permute-done.1 = f32[640,512]{1,0:T(8,128)} collective-permute-done((f32[640,512]{1,0:T(8,128)S(1)}, f32[640,512]{1,0:T(8,128)}, u32[]{:S(2)}, u32[]{:S(2)}) %collective-permute-start.1) | collective-permute-done | bytes 1310752 | tf_op jit(solution)/shard_map/ppermute | solution.py:10
  161.7 1.3 collective-permute-start.2
  163.0 0.0 all-gather.2.cloned.1.call-done
  163.0 3.6 %slice_bitcast_fusion = (f32[512,512]{1,0:T(8,128)}, f32[512,512]{1,0:T(8,128)}, f32[512,512]{1,0:T(8,128)S(1)}) fusion(f32[512,2048]{0,1:T(8,128)} %all-gather.2.cloned.1.call-done), kind=kLoop, calls=%fused_computation.7 | loop fusion | bytes 6291456 | tf_op jit(solution)/shard_map/transpose | solution.py:35
  166.6 27.9 %collective-permute-done.2 = f32[640,512]{1,0:T(8,128)} collective-permute-done((f32[640,512]{1,0:T(8,128)}, f32[640,512]{1,0:T(8,128)}, u32[]{:S(2)}, u32[]{:S(2)}) %collective-permute-start.2) | collective-permute-done | bytes 1310752 | tf_op jit(solution)/shard_map/ppermute | solution.py:10
  194.5 3.7 %conditional.13 = (f32[640,512]{1,0:T(8,128)S(1)}) conditional(s32[]{:T(128)} %convert_element_type.8, f32[640,512]{1,0:T(8,128)S(1)} %get-tuple-element.132, (f32[640,512]{1,0:T(8,128)}, f32[512,512]{1,0:T(8,128)S(1)}, f32[640,512]{1,0:T(8,128)S(1)}) %tuple.71), branch_computations={%region_6.0_spmd, %region_7.0_spmd} | conditional | flops 2013593600 | bytes 4980744 | solution.py:39
  194.5 3.7 %convolution_subtract_fusion.2 = f32[640,512]{1,0:T(8,128)S(1)} fusion(f32[640,512]{1,0:T(8,128)S(1)} %get-tuple-element.106, f32[640,512]{1,0:T(8,128)} %get-tuple-element.107, f32[512,512]{1,0:T(8,128)S(1)} %get-tuple-element.108), kind=kOutput, calls=%fused_computation.2 | convolution fusion | flops 2013593600 | bytes 4980736 | tf_op jit(solution)/shard_map/cond/branch_1_fun/dot_general | solution.py:14
  198.2 0.0 copy-start
  198.2 1.4 collective-permute-start.3
  199.7 29.0 %collective-permute-done.3 = f32[640,512]{1,0:T(8,128)} collective-permute-done((f32[640,512]{1,0:T(8,128)}, f32[640,512]{1,0:T(8,128)}, u32[]{:S(2)}, u32[]{:S(2)}) %collective-permute-start.3) | collective-permute-done | bytes 1310752 | tf_op jit(solution)/shard_map/ppermute | solution.py:10
  228.7 1.3 collective-permute-start.4
  230.0 0.0 copy-done
  230.0 28.1 %collective-permute-done.4 = f32[640,512]{1,0:T(8,128)} collective-permute-done((f32[640,512]{1,0:T(8,128)}, f32[640,512]{1,0:T(8,128)}, u32[]{:S(2)}, u32[]{:S(2)}) %collective-permute-start.4) | collective-permute-done | bytes 1310752 | tf_op jit(solution)/shard_map/ppermute | solution.py:10
  258.1 3.7 %conditional.16 = (f32[640,512]{1,0:T(8,128)S(1)}) conditional(s32[]{:T(128)} %convert_element_type.8, f32[640,512]{1,0:T(8,128)S(1)} %get-tuple-element.135, (f32[640,512]{1,0:T(8,128)}, f32[512,512]{1,0:T(8,128)S(1)}, f32[640,512]{1,0:T(8,128)S(1)}) %tuple.111), branch_computations={%region_12.0_spmd, %region_13.0_spmd} | conditional | flops 2013593600 | bytes 4980744 | solution.py:39
  258.1 3.7 %convolution_subtract_fusion.4 = f32[640,512]{1,0:T(8,128)S(1)} fusion(f32[640,512]{1,0:T(8,128)S(1)} %get-tuple-element.114, f32[640,512]{1,0:T(8,128)} %get-tuple-element.115, f32[512,512]{1,0:T(8,128)S(1)} %get-tuple-element.116), kind=kOutput, calls=%fused_computation.4 | convolution fusion | flops 2013593600 | bytes 4980736 | tf_op jit(solution)/shard_map/cond/branch_1_fun/dot_general | solution.py:14
  261.8 0.0 copy-start.1
  261.8 1.4 collective-permute-start.5
  263.3 27.2 %collective-permute-done.5 = f32[640,512]{1,0:T(8,128)S(1)} collective-permute-done((f32[640,512]{1,0:T(8,128)}, f32[640,512]{1,0:T(8,128)S(1)}, u32[]{:S(2)}, u32[]{:S(2)}) %collective-permute-start.5) | collective-permute-done | bytes 1310752 | tf_op jit(solution)/shard_map/ppermute | solution.py:10
  290.4 0.0 copy-done.1
  290.4 4.8 %conditional.18 = (f32[640,512]{1,0:T(8,128)S(1)}) conditional(s32[]{:T(128)} %convert_element_type.8, f32[640,512]{1,0:T(8,128)S(1)} %get-tuple-element.136, (f32[640,512]{1,0:T(8,128)S(1)}, f32[512,512]{1,0:T(8,128)S(1)}, f32[640,512]{1,0:T(8,128)S(1)}) %tuple.112), branch_computations={%region_16.0_spmd, %region_17.0_spmd} | conditional | flops 2013593600 | bytes 10223652 | solution.py:39
  290.4 0.0 copy-start.4
  290.4 1.1 copy-done.4
  291.5 3.7 %convolution_subtract_fusion.5 = f32[640,512]{1,0:T(8,128)S(1)} fusion(f32[640,512]{1,0:T(8,128)S(1)} %get-tuple-element.119, f32[640,512]{1,0:T(8,128)} %copy-done.4, f32[512,512]{1,0:T(8,128)S(1)} %get-tuple-element.121), kind=kOutput, calls=%fused_computation.5 | convolution fusion | flops 2013593600 | bytes 4980736 | tf_op jit(solution)/shard_map/cond/branch_1_fun/dot_general | solution.py:14
  295.2 3.3 %conditional.19 = (f32[1,640,512]{2,1,0:T(8,128)}) conditional(s32[]{:T(128)} %convert_element_type.8, f32[640,512]{1,0:T(8,128)} %get-tuple-element.137, (f32[640,512]{1,0:T(8,128)S(1)}, f32[512,512]{1,0:T(8,128)S(1)}) %tuple.109), branch_computations={%region_18.0_spmd, %region_19.0_spmd} | conditional | flops 2013265920 | bytes 3670024 | solution.py:33
  295.3 3.3 %convolution_bitcast_fusion = f32[1,640,512]{2,1,0:T(8,128)} fusion(f32[640,512]{1,0:T(8,128)S(1)} %get-tuple-element.122, f32[512,512]{1,0:T(8,128)S(1)} %get-tuple-element.123), kind=kOutput, calls=%fused_computation.6 | convolution fusion | flops 2013265920 | bytes 3670016 | tf_op jit(solution)/shard_map/cond/branch_1_fun/dot_general | solution.py:14
  (5 shorter events, 0.0 us)
Async XLA Ops:
  6.5 2.2 copy-start.2
  6.5 156.5 %all-gather.2.cloned.1.call-start = ((), (), s32[]{:S(2)}) async-start(), calls=%async_computation.2 | async-start | bytes 4718592 | tf_op jit(solution)/shard_map/all_gather | solution.py:27
  39.7 5.2 %copy-start.5 = (f32[1,512,512]{2,1,0:T(8,128)S(1)}, f32[1,512,512]{2,1,0:T(8,128)}, u32[]{:S(2)}) copy-start(f32[1,512,512]{2,1,0:T(8,128)} %param.25) | copy-start | bytes 3145732
  39.7 50.6 %all-to-all-start.1 = ((f32[1,160,2048]{1,0,2:T(1,128)}), f32[1,160,2048]{1,0,2:T(1,128)}, u32[]{:S(2)}, u32[]{:S(2)}) async-start(f32[1,160,2048]{1,0,2:T(1,128)} %reshape.15), calls=%async_computation.1 | async-start | bytes 4194304 | tf_op jit(solution)/shard_map/all_to_all | solution.py:18
  99.7 30.9 %collective-permute-start = (f32[640,512]{1,0:T(8,128)}, f32[640,512]{1,0:T(8,128)S(1)}, u32[]{:S(2)}, u32[]{:S(2)}) collective-permute-start(f32[640,512]{1,0:T(8,128)} %get-tuple-element.130), channel_id=1, source_target_pairs={{0,1},{1,2},{2,3},{4,5},{5,6},{6,7},{8,9},{9,10},{10,11},{12,13},{... | collective-permute-start | bytes 3932168 | tf_op jit(solution)/shard_map/ppermute | solution.py:10
  130.6 1.1 copy-start.3
  131.7 30.0 %collective-permute-start.1 = (f32[640,512]{1,0:T(8,128)S(1)}, f32[640,512]{1,0:T(8,128)}, u32[]{:S(2)}, u32[]{:S(2)}) collective-permute-start(f32[640,512]{1,0:T(8,128)S(1)} %collective-permute-done), channel_id=1, source_target_pairs={{0,1},{1,2},{2,3},{4,5},{5,6},{6,7},{8,9},{9,10},{10,11},{12,13},{... | collective-permute-start | bytes 3932168 | tf_op jit(solution)/shard_map/ppermute | solution.py:10
  161.7 32.8 %collective-permute-start.2 = (f32[640,512]{1,0:T(8,128)}, f32[640,512]{1,0:T(8,128)}, u32[]{:S(2)}, u32[]{:S(2)}) collective-permute-start(f32[640,512]{1,0:T(8,128)} %collective-permute-done.1), channel_id=1, source_target_pairs={{0,1},{1,2},{2,3},{4,5},{5,6},{6,7},{8,9},{9,10},{10,11},{12,13},{... | collective-permute-start | bytes 3932168 | tf_op jit(solution)/shard_map/ppermute | solution.py:10
  198.2 31.7 %copy-start = (f32[512,512]{1,0:T(8,128)S(1)}, f32[512,512]{1,0:T(8,128)}, u32[]{:S(2)}) copy-start(f32[512,512]{1,0:T(8,128)} %get-tuple-element.126) | copy-start | bytes 3145732
  198.2 30.4 %collective-permute-start.3 = (f32[640,512]{1,0:T(8,128)}, f32[640,512]{1,0:T(8,128)}, u32[]{:S(2)}, u32[]{:S(2)}) collective-permute-start(f32[640,512]{1,0:T(8,128)} %get-tuple-element.134), channel_id=1, source_target_pairs={{0,1},{1,2},{2,3},{4,5},{5,6},{6,7},{8,9},{9,10},{10,11},{12,13},{... | collective-permute-start | bytes 3932168 | tf_op jit(solution)/shard_map/ppermute | solution.py:10
  228.7 29.4 %collective-permute-start.4 = (f32[640,512]{1,0:T(8,128)}, f32[640,512]{1,0:T(8,128)}, u32[]{:S(2)}, u32[]{:S(2)}) collective-permute-start(f32[640,512]{1,0:T(8,128)} %collective-permute-done.3), channel_id=1, source_target_pairs={{0,1},{1,2},{2,3},{4,5},{5,6},{6,7},{8,9},{9,10},{10,11},{12,13},{... | collective-permute-start | bytes 3932168 | tf_op jit(solution)/shard_map/ppermute | solution.py:10
  261.8 28.6 %copy-start.1 = (f32[512,512]{1,0:T(8,128)S(1)}, f32[512,512]{1,0:T(8,128)}, u32[]{:S(2)}) copy-start(f32[512,512]{1,0:T(8,128)} %get-tuple-element.125) | copy-start | bytes 3145732
  261.8 28.6 %collective-permute-start.5 = (f32[640,512]{1,0:T(8,128)}, f32[640,512]{1,0:T(8,128)S(1)}, u32[]{:S(2)}, u32[]{:S(2)}) collective-permute-start(f32[640,512]{1,0:T(8,128)} %get-tuple-element.137), channel_id=1, source_target_pairs={{0,1},{1,2},{2,3},{4,5},{5,6},{6,7},{8,9},{9,10},{10,11},{12,13},{... | collective-permute-start | bytes 3932168 | tf_op jit(solution)/shard_map/ppermute | solution.py:10
  290.4 1.1 copy-start.4
Sparse Core Ops, SparseCore 0:
  9.2 45.3 all-gather.1
where the time goes:
time: 308 us; the launch traced here: 305 us
  waiting for transfers between devices  216 us (70%)
  blocking collectives  25.5 us (8%)
  local copies, waits for them, and re-layouts  23.1 us (8%)
  matrix products  14.5 us (5%)
  between operations  13.6 us (4%)
  starting transfers between devices  13.2 us (4%)
    ppermute x6, waiting for transfers between devices, from_behind(): return lax.ppermute(block, axis, route)  170 us
    all_to_all x1, waiting for transfers between devices, local(): lax.all_to_all(lax.all_to_all(integrals, 'pair', split_axis=0, concat_axi...  45 us
    all_to_all x1, blocking collectives, local(): lax.all_to_all(integrals, 'pair', split_axis=0, concat_axis=2, tiled=True)  25.5 us
    dot_general x4, matrix products, product(): jnp.dot(left, right, precision=lax.Precision.HIGHEST, preferred_element_t...  14.5 us
    all_to_all x3, local copies, waits for them, and re-layouts, local(): lax.all_to_all(lax.all_to_all(integrals, 'pair', split_axis=0, concat_axi...  8.11 us
    ppermute x6, starting transfers between devices, from_behind(): return lax.ppermute(block, axis, route)  7.97 us
  transfers between devices with their start and end apart: 8, of which 7 were waited for; matrix products, arithmetic and copies ran while one was open for 5% of the time, Pallas kernels for 0%

commit v1 on v0

v1 whole, which is shorter than its diff:
```python
import functools

import jax
import jax.numpy as jnp
from jax import lax
from jax.experimental import pallas as pl
from jax.experimental.pallas import tpu as pltpu
from jax.sharding import PartitionSpec as P

MESH = pl.DeviceIdType.MESH


def flip(index, mask):
    result = index
    bit = 1
    while bit <= mask:
        if mask & bit:
            result = result + bit * (1 - 2 * ((index // bit) % 2))
        bit *= 2
    return result


def subsets(bits):
    found = [0]
    for bit in bits:
        found = found + [m | bit for m in found]
    return found


def halves_of(value):
    high = value.astype(jnp.bfloat16)
    low = (value - high.astype(jnp.float32)).astype(jnp.bfloat16)
    return high, low


def dot_t(left, right):
    return lax.dot_general(left, right, (((1,), (1,)), ((), ())), preferred_element_type=jnp.float32)


def product(left, right):
    return dot_t(left[0], right[0]) + (dot_t(left[0], right[1]) + dot_t(left[1], right[0]))


def kernel(pairs, panels, integrals, own, out, rows_in, weights, solved, high, low, total,
           own_sem, act_send, act_recv, z_send, z_recv, w_send, w_recv, out_send, out_recv):
    p = lax.axis_index("pair")
    z = lax.axis_index("aux")
    each = pairs // panels
    width, cols = own.shape
    occ = rows_in.shape[1]
    virt = rows_in.shape[2]
    rows = occ * virt
    half = width // 2
    bits = [1 << b for b in range(1, pairs.bit_length() - 1)]
    orders = (bits, bits[::-1])
    stages = len(bits)

    def low_of(j):
        return pairs - each if j == 0 else 0

    def base(j):
        return each * (j * (j + 1) // 2)

    def held(j, q):
        return jnp.logical_and(q >= low_of(j), q < low_of(j) + (j + 1) * each)

    def slot(j, q):
        return base(j) + q - low_of(j)

    def on(condition, action):
        pl.when(condition)(action)

    barrier = pltpu.get_barrier_semaphore()
    for m in range(1, pairs):
        pl.semaphore_signal(barrier, inc=1, device_id={"pair": flip(p, m)}, device_id_type=MESH)
    for d in range(1, panels):
        pl.semaphore_signal(barrier, inc=1, device_id={"aux": (z + d) % panels}, device_id_type=MESH)

    def own_copy(j):
        return pltpu.make_async_copy(own, weights.at[slot(j, p)], own_sem.at[0])

    own_rows = pltpu.make_async_copy(integrals.at[pl.ds(p * occ, occ)], rows_in.at[p], own_sem.at[1])
    own_rows.start()
    for j in range(panels):
        on(jnp.logical_and(z == j, held(j, p)), lambda j=j: own_copy(j).start())
    for j in range(panels):
        on(jnp.logical_and(z == j, held(j, p)), lambda j=j: own_copy(j).wait())
    pl.semaphore_wait(barrier, pairs - 1 + panels - 1)

    def z_copy(j, way):
        ref = weights.at[slot(j, p)]
        step = 1 if way else -1
        return pltpu.make_async_remote_copy(
            ref, ref, z_send.at[j, way], z_recv.at[j], device_id={"aux": z + step}, device_id_type=MESH)

    def z_sends(j, way, source):
        edge = z < panels - 1 if way else z > 0
        side = z == j if source else (z > j if way else z < j)
        return jnp.logical_and(jnp.logical_and(edge, side), held(j, p))

    for j in range(panels):
        for way in range(2):
            on(z_sends(j, way, True), lambda j=j, way=way: z_copy(j, way).start())

    def act_copy(m):
        target = flip(p, m)
        return pltpu.make_async_remote_copy(
            integrals.at[pl.ds(target * occ, occ)], rows_in.at[p], act_send.at[m], act_recv.at[m],
            device_id={"pair": target}, device_id_type=MESH)

    for m in range(1, pairs):
        act_copy(m).start()

    def w_copy(j, h, rel, bit):
        ref = weights.at[slot(j, flip(p, rel ^ bit)), pl.ds(h * half, half)]
        return pltpu.make_async_remote_copy(
            ref, ref, w_send.at[j, h, rel], w_recv.at[j, h, rel],
            device_id={"pair": flip(p, bit)}, device_id_type=MESH)

    sent = []

    def w_start(j, h, m, bit):
        on(held(j, flip(p, m)), lambda: w_copy(j, h, m ^ bit, bit).start())
        sent.append((j, h, m, bit))

    def w_wait(j, h, rel):
        ref = weights.at[slot(j, flip(p, rel)), pl.ds(h * half, half)]

        def wait():
            pltpu.make_async_remote_copy(
                ref, ref, w_send.at[j, h, rel], w_recv.at[j, h, rel],
                device_id={"pair": flip(p, 1)}, device_id_type=MESH).wait_recv()

        on(held(j, flip(p, rel)), wait)

    def stage(j, s):
        for h in range(2):
            for m in subsets(orders[h][:s]):
                w_start(j, h, m, orders[h][s])

    def stage_wait(j, s):
        for h in range(2):
            for m in subsets(orders[h][:s]):
                w_wait(j, h, m ^ orders[h][s])
                w_start(j, h, m ^ orders[h][s], 1)

    for j in range(panels):
        on(jnp.logical_and(z != j, held(j, p)), lambda j=j: z_copy(j, 0).wait_recv())
        for way in range(2):
            on(z_sends(j, way, False), lambda j=j, way=way: z_copy(j, way).start())
        stage(j, 0)
        for h in range(2):
            w_start(j, h, 0, 1)

    own_rows.wait()
    for m in range(1, pairs):
        act_copy(m).wait_recv()

    def out_copy(j):
        return pltpu.make_async_remote_copy(
            solved.at[j], out.at[:, pl.ds(pl.multiple_of(z * virt, 8), virt)], out_send.at[j], out_recv.at[z],
            device_id={"aux": j}, device_id_type=MESH)

    def keep_copy(j):
        return pltpu.make_async_copy(
            solved.at[j], out.at[:, pl.ds(pl.multiple_of(z * virt, 8), virt)], out_send.at[j])

    def solve(j):
        if j:
            total[...] = jnp.zeros_like(total)

            def add(q, carry):
                total[...] += product((high[q], low[q]), halves_of(weights[base(j) + q]))
                return carry

            lax.fori_loop(0, j * each, add, 0)
        answer = None
        for t in range(each):
            remain = rows_in[j * each + t].reshape(rows, cols)
            if j:
                remain = remain - total[:, t * cols:(t + 1) * cols]
            term = product(halves_of(remain), halves_of(weights[base(j) + j * each + t]))
            answer = term if answer is None else answer + term
        solved[j] = answer.reshape(occ, virt, width)
        if j + 1 < panels:
            for t in range(each):
                high_t, low_t = halves_of(answer[:, t * cols:(t + 1) * cols])
                high[j * each + t] = high_t
                low[j * each + t] = low_t
        on(z != j, lambda: out_copy(j).start())
        on(z == j, lambda: keep_copy(j).start())

    for j in range(panels + 1):
        if j < panels:
            for s in range(1, stages):
                stage_wait(j, s - 1)
                stage(j, s)
        if j:
            stage_wait(j - 1, stages - 1)
            for h in range(2):
                for m in subsets(bits):
                    w_wait(j - 1, h, m ^ 1)
            solve(j - 1)

    for m in range(1, pairs):
        act_copy(m).wait_send()
    for j in range(panels):
        for way in range(2):
            on(jnp.logical_or(z_sends(j, way, True), z_sends(j, way, False)),
               lambda j=j, way=way: z_copy(j, way).wait_send())
    for j, h, m, bit in sent:
        on(held(j, flip(p, m)), lambda j=j, h=h, m=m, bit=bit: w_copy(j, h, m ^ bit, bit).wait_send())
    for j in range(panels):
        on(z == j, lambda j=j: keep_copy(j).wait())
        on(z != j, lambda j=j: out_copy(j).wait_send())

    def out_wait(source):
        pltpu.make_async_remote_copy(
            solved.at[0], out.at[:, pl.ds(source * virt, virt)], out_send.at[0], out_recv.at[source],
            device_id={"aux": (z + 1) % panels}, device_id_type=MESH).wait_recv()

    for source in range(panels):
        on(z != source, lambda source=source: out_wait(source))


def local(integrals, factor, diag_inverse):
    pairs = lax.axis_size("pair")
    panels = lax.axis_size("aux")
    p = lax.axis_index("pair")
    z = lax.axis_index("aux")
    width, cols = factor.shape
    occ_all, virt, _ = integrals.shape
    each = pairs // panels
    occ = occ_all // pairs
    t = jnp.where(z == 0, p - (pairs - each), p - z * each)
    inside = jnp.logical_and(t >= 0, t < each)
    own_diag = lax.dynamic_slice(diag_inverse[0], (0, jnp.clip(t, 0, each - 1) * cols), (width, cols))
    own = jnp.where(inside, own_diag, factor)
    vmem = pl.BlockSpec(memory_space=pltpu.VMEM)
    dma = pltpu.SemaphoreType.DMA
    blocks = each * panels * (panels + 1) // 2
    return pl.pallas_call(
        functools.partial(kernel, pairs, panels),
        out_shape=jax.ShapeDtypeStruct((occ, virt * panels, width), jnp.float32),
        in_specs=[vmem, vmem],
        out_specs=vmem,
        scratch_shapes=[
            pltpu.VMEM((pairs, occ, virt, cols), jnp.float32),
            pltpu.VMEM((blocks, width, cols), jnp.float32),
            pltpu.VMEM((panels, occ, virt, width), jnp.float32),
            pltpu.VMEM((pairs, occ * virt, cols), jnp.bfloat16),
            pltpu.VMEM((pairs, occ * virt, cols), jnp.bfloat16),
            pltpu.VMEM((occ * virt, width), jnp.float32),
            dma((2,)),
            dma((pairs,)),
            dma((pairs,)),
            dma((panels, 2)),
            dma((panels,)),
            dma((panels, 2, pairs)),
            dma((panels, 2, pairs)),
            dma((panels,)),
            dma((panels,)),
        ],
        compiler_params=pltpu.CompilerParams(
            collective_id=0, has_side_effects=True, vmem_limit_bytes=60 * 1024 * 1024),
    )(integrals, own)


def solution(mesh):
    in_specs = (P(None, "aux", "pair"), P("aux", "pair"), P("aux", None, None))
    out_specs = P("pair", None, "aux")
    return jax.shard_map(local, mesh=mesh, in_specs=in_specs, out_specs=out_specs, check_vma=False)
```

time: 308 us -> 126 us (0.41)
  waiting for transfers between devices: 216 us -> 0 us
  Pallas kernels: 0 us -> 122 us
  blocking collectives: 25.5 us -> 0 us
  local copies, waits for them, and re-layouts: 23.1 us -> 2.47 us
  matrix products: 14.5 us -> 0 us
  between operations: 13.6 us -> 0.01 us
  starting transfers between devices: 13.2 us -> 0 us
    ppermute x6 -> x0, waiting for transfers between devices: 170 us -> none  [from_behind(): return lax.ppermute(block, axis, route)]
    pallas_call x0 -> x1, Pallas kernels: none -> 122 us  [local(): pl.pallas_call(functools.partial(kernel, pairs, panels), out_shape=jax.Sh...]
    all_to_all x1 -> x0, waiting for transfers between devices: 45 us -> none  [local(): lax.all_to_all(lax.all_to_all(integrals, 'pair', split_axis=0, concat_axi...]
    all_to_all x1 -> x0, blocking collectives: 25.5 us -> none  [local(): lax.all_to_all(integrals, 'pair', split_axis=0, concat_axis=2, tiled=True)]
    dot_general x4 -> x0, matrix products: 14.5 us -> none  [product(): jnp.dot(left, right, precision=lax.Precision.HIGHEST, preferred_element_t...]
    all_to_all x5 -> x0, local copies, waits for them, and re-layouts: 13.6 us -> none  [the longest x3 8.11 us: local(): lax.all_to_all(lax.all_to_all(integrals, 'pair', split_axis=0, concat_axi...]
    ppermute x6 -> x0, starting transfers between devices: 7.97 us -> none  [from_behind(): return lax.ppermute(block, axis, route)]
    all_to_all x1 -> x0, starting transfers between devices: 5.22 us -> none  [local(): lax.all_to_all(lax.all_to_all(integrals, 'pair', split_axis=0, concat_axi...]
  transfers between devices with their start and end apart: 8 -> 0, of which waited for: 7 -> 0; matrix products, arithmetic and copies ran while one was open for 5% -> 0% of each run, Pallas kernels for 0% -> 0%
where the time goes in v1:
time: 126 us
  Pallas kernels  122 us (97%)
  local copies, waits for them, and re-layouts  2.47 us (2%)
  other arithmetic  1.9 us (2%)
    pallas_call x1, Pallas kernels, local(): pl.pallas_call(functools.partial(kernel, pairs, panels), out_shape=jax.Sh...  122 us

profile of v1, /device:TPU:30, one launch (start us, length us, event | category | flops | bytes accessed | tf_op | source)
XLA Modules:
  0.0 126.3 jit_solution(5306044385022448140)
XLA Ops:
  0.0 1.9 %bitcast_select_fusion.own = f32[512,256]{1,0:T(8,128)} fusion(f32[512,256]{1,0:T(8,128)} %param.4, f32[1,512,512]{2,1,0:T(8,128)} %param.5, s32[]{:T(128)S(6)} %select_n.17, pred[]{:T(512)S(6)} %and.5), kind=kLoop, calls=%fused_computation | loop fusion | flops 131072 | bytes 1572869 | tf_op jit(solution)/shard_map/jit(_where)/select_n | solution.py:238
  1.9 121.9 %shard_map.37 = f32[1,640,512]{2,1,0:T(8,128)} custom-call(f32[8,160,256]{2,1,0:T(8,128)} %integrals.1, f32[512,256]{1,0:T(8,128)} %bitcast_select_fusion.own), custom_call_target="tpu_custom_call" | custom-call | tf_op jit(solution)/shard_map/pallas_call | solution.py:242
  123.8 2.5 %copy.5 = f32[1,640,512]{2,1,0:T(8,128)} copy(f32[1,640,512]{2,1,0:T(8,128)} %shard_map.37) | data formatting | bytes 2621440
